TPU v7x, 32 devices: a whole 2x2x4 slice. The times are simulated.
32 devices in a mesh: row: 4 (over z), col: 8 (over y, x, core).
Axes of the slice: x: 2, y: 2, z: 4, core: 2. Of those that a mesh axis runs over, the one named last changes fastest.
Arguments:
- factor: bfloat16 [32768, 5, 1024], P('col', None, 'row'), may hold values from -0.0625 to 0.0625
- diag_inverse: bfloat16 [5, 1024, 1024], P(None, 'row'), may hold values from -1 to 2
- right_side: float32 [16, 32, 1024], P(None, 'col', 'row'), may hold values from -6 to 6
- tile_order: int32 [32], replicated, may hold values from 0 to 31, each once
- live_segments: int32 [16], replicated, may hold values from 2 to 5
Outputs:
- result: float32 [16, 32, 1024], P(None, 'col', 'row')
Inputs may be any that keep to these rules, and one draw needn't show every extreme that they name: `tile_order`: each of 0 to 31 appears once.
All inputs are finite; a program needn't handle non-finite values.
Results may differ from a plain program's by a relative error of at most 0.0019.
Values may be sent and summed in bfloat16 or wider, within the bound.
A program may use at most 64 MiB of HBM per device.

v0:
```python
import jax
import jax.numpy as jnp
from jax import lax
from jax.sharding import PartitionSpec as P


def spread(block, axis, owner):
    block = jnp.where(lax.axis_index(axis) == owner, block, jnp.zeros_like(block))
    return lax.psum(block, axis)


def per_device(factor, diag_inverse, right_side, tile_order, live_segments):
    section_count = diag_inverse.shape[0]
    slice_width = diag_inverse.shape[1]
    tile_width = diag_inverse.shape[2]
    rhs_count = right_side.shape[0]
    rows_dev = right_side.shape[1]
    my_col = lax.axis_index("col")
    my_row = lax.axis_index("row")
    slice_start = my_row * slice_width
    partial_value = jnp.zeros((rhs_count, rows_dev * tile_width), jnp.float32)
    result = jnp.zeros((rhs_count, rows_dev, slice_width), jnp.float32)
    for section in range(section_count):
        slot_id = tile_order[section]
        root_col = slot_id // rows_dev
        local_pos = slot_id % rows_dev
        part_tile = lax.dynamic_slice_in_dim(partial_value, local_pos * tile_width, tile_width, 1)
        rhs_slice = lax.dynamic_index_in_dim(right_side, local_pos, 1, keepdims=False)
        placed = lax.dynamic_update_slice_in_dim(
            jnp.zeros((rhs_count, tile_width), jnp.float32), rhs_slice, slice_start, 1
        )
        remaining = lax.psum(placed - part_tile, "row")
        inverse = diag_inverse[section].astype(jnp.float32)
        solved = lax.dot_general(
            remaining,
            inverse,
            (((1,), (1,)), ((), ())),
            precision=lax.Precision.HIGHEST,
            preferred_element_type=jnp.float32,
        )
        is_live = (section < live_segments)[:, None]
        sent_block = jnp.where(is_live, solved, jnp.zeros_like(solved)).astype(jnp.bfloat16)
        sent_block = spread(sent_block, "col", root_col)
        kept_part = lax.dynamic_slice_in_dim(remaining, slice_start, slice_width, 1)
        stored = jnp.where(is_live, solved, kept_part)
        written = lax.dynamic_update_slice_in_dim(result, stored[:, None, :], local_pos, 1)
        result = jnp.where(my_col == root_col, written, result)
        panel_rows = factor[:, section, :]
        partial_value = partial_value + lax.dot_general(
            sent_block, panel_rows, (((1,), (1,)), ((), ())), preferred_element_type=jnp.float32
        )
    shaped = partial_value.reshape(rhs_count, rows_dev, tile_width)
    total_part = lax.psum_scatter(shaped, "row", scatter_dimension=2, tiled=True)
    local_slots = my_col * rows_dev + jnp.arange(rows_dev, dtype=jnp.int32)
    visited = jnp.any(local_slots[:, None] == tile_order[:section_count][None, :], axis=1)
    return jnp.where(visited[None, :, None], result, right_side - total_part)


def solution(mesh):
    return jax.shard_map(
        per_device,
        mesh=mesh,
        in_specs=(P("col", None, "row"), P(None, "row", None), P(None, "col", "row"), P(), P()),
        out_specs=P(None, "col", "row"),
        check_vma=False,
    )
```

profile of v0, /device:TPU:0, one launch (start us, length us, event | category | flops | bytes accessed | tf_op | source)
XLA Modules:
  0.0 292.0 jit_solution(3287406973859240953)
XLA Ops:
  6.5 1.5 fusion.35
  10.1 0.9 copy.16
  22.0 26.9 %all-reduce.6.cloned.1.call-done = f32[16,1024]{1,0:T(8,128)} async-done(((f32[16,1024]{1,0:T(8,128)}), f32[16,1024]{1,0:T(8,128)}) %all-reduce.6.cloned.1.call-update) | async-done | bytes 65552 | tf_op jit(solution)/shard_map/psum | solution.py:32
  48.9 1.6 bitcast_dynamic-update-slice_fusion.4
  50.5 12.1 %psum.71 = bf16[16,256]{1,0:T(8,128)(2,1)S(1)} all-reduce(bf16[16,256]{1,0:T(8,128)(2,1)S(1)} %fusion.30), channel_id=1, replica_groups=mesh['row'=4,'col'=8] {'col'}, use_global_device_ids=true, to_apply=%region_2.3 | all-reduce | flops 4096 | bytes 16384 | tf_op jit(solution)/shard_map/psum | solution.py:9
  62.7 2.2 fusion.4
  65.7 33.1 %all-reduce.8.cloned.1.call-done = f32[16,1024]{1,0:T(8,128)} async-done(((f32[16,1024]{1,0:T(8,128)}), f32[16,1024]{1,0:T(8,128)}) %all-reduce.8.cloned.1.call-update) | async-done | bytes 65552 | tf_op jit(solution)/shard_map/psum | solution.py:32
  98.8 1.4 fusion.29
  100.3 12.1 %psum.73 = bf16[16,256]{1,0:T(8,128)(2,1)S(1)} all-reduce(bf16[16,256]{1,0:T(8,128)(2,1)S(1)} %fusion.31), channel_id=1, replica_groups=mesh['row'=4,'col'=8] {'col'}, use_global_device_ids=true, to_apply=%region_4.5 | all-reduce | flops 4096 | bytes 16384 | tf_op jit(solution)/shard_map/psum | solution.py:9
  112.4 2.2 convolution_add_fusion.3
  115.4 33.1 %all-reduce.10.cloned.1.call-done = f32[16,1024]{1,0:T(8,128)} async-done(((f32[16,1024]{1,0:T(8,128)}), f32[16,1024]{1,0:T(8,128)}) %all-reduce.10.cloned.1.call-update) | async-done | bytes 65552 | tf_op jit(solution)/shard_map/psum | solution.py:32
  148.5 1.4 fusion.28
  150.0 12.1 %psum.75 = bf16[16,256]{1,0:T(8,128)(2,1)S(1)} all-reduce(bf16[16,256]{1,0:T(8,128)(2,1)S(1)} %fusion.32), channel_id=1, replica_groups=mesh['row'=4,'col'=8] {'col'}, use_global_device_ids=true, to_apply=%region_6.7 | all-reduce | flops 4096 | bytes 16384 | tf_op jit(solution)/shard_map/psum | solution.py:9
  162.1 2.2 convolution_add_fusion.2
  165.1 33.1 %all-reduce.12.cloned.1.call-done = f32[16,1024]{1,0:T(8,128)} async-done(((f32[16,1024]{1,0:T(8,128)}), f32[16,1024]{1,0:T(8,128)}) %all-reduce.12.cloned.1.call-update) | async-done | bytes 65552 | tf_op jit(solution)/shard_map/psum | solution.py:32
  198.3 1.4 fusion.27
  199.7 12.1 %psum.77 = bf16[16,256]{1,0:T(8,128)(2,1)S(1)} all-reduce(bf16[16,256]{1,0:T(8,128)(2,1)S(1)} %fusion.33), channel_id=1, replica_groups=mesh['row'=4,'col'=8] {'col'}, use_global_device_ids=true, to_apply=%region_8.9 | all-reduce | flops 4096 | bytes 16384 | tf_op jit(solution)/shard_map/psum | solution.py:9
  211.9 2.2 convolution_add_fusion.1
  215.5 32.5 %all-reduce.14.cloned.1.call-done = f32[16,1024]{1,0:T(8,128)} async-done(((f32[16,1024]{1,0:T(8,128)}), f32[16,1024]{1,0:T(8,128)}) %all-reduce.14.cloned.1.call-update) | async-done | bytes 65552 | tf_op jit(solution)/shard_map/psum | solution.py:32
  248.0 1.4 fusion.26
  249.5 12.1 %psum.79 = bf16[16,256]{1,0:T(8,128)(2,1)S(1)} all-reduce(bf16[16,256]{1,0:T(8,128)(2,1)S(1)} %fusion.34), channel_id=1, replica_groups=mesh['row'=4,'col'=8] {'col'}, use_global_device_ids=true, to_apply=%region_10.11 | all-reduce | flops 4096 | bytes 16384 | tf_op jit(solution)/shard_map/psum | solution.py:9
  261.6 2.2 convolution_add_fusion
  264.8 18.8 %reduce-scatter.2.cloned.1.call-done = f32[16,4,256]{2,0,1:T(8,128)} async-done(((f32[16,4,1024]{2,0,1:T(8,128)}), f32[16,4,256]{2,0,1:T(8,128)}) %reduce-scatter.2.cloned.1.call-update) | async-done | bytes 65552 | tf_op jit(solution)/shard_map/reduce_scatter | solution.py:53
  283.5 0.9 subtract_select_fusion
  (45 shorter events, 6.3 us)
Async XLA Ops:
  6.5 92.3 %copy-start = (bf16[5,256,1024]{2,1,0:T(8,128)(2,1)S(1)}, bf16[5,256,1024]{2,1,0:T(8,128)(2,1)}, u32[]{:S(2)}) copy-start(bf16[5,256,1024]{2,1,0:T(8,128)(2,1)} %param.6) | copy-start | bytes 7864324
  6.5 42.3 %all-reduce.6.cloned.1.call-start = ((), (), s32[]{:S(2)}) async-start(), calls=%async_computation.1 | async-start | bytes 131072 | tf_op jit(solution)/shard_map/psum | solution.py:32
  11.0 0.6 copy-start.1
  11.7 87.1 %all-reduce.8.cloned.1.call-start = ((), (), s32[]{:S(2)}) async-start(), calls=%async_computation.2 | async-start | bytes 131072 | tf_op jit(solution)/shard_map/psum | solution.py:32
  65.6 83.0 %all-reduce.10.cloned.1.call-start = ((), (), s32[]{:S(2)}) async-start(), calls=%async_computation.3 | async-start | bytes 131072 | tf_op jit(solution)/shard_map/psum | solution.py:32
  115.3 83.0 %all-reduce.12.cloned.1.call-start = ((), (), s32[]{:S(2)}) async-start(), calls=%async_computation.4 | async-start | bytes 131072 | tf_op jit(solution)/shard_map/psum | solution.py:32
  165.0 83.0 %all-reduce.14.cloned.1.call-start = ((), (), s32[]{:S(2)}) async-start(), calls=%async_computation.5 | async-start | bytes 131072 | tf_op jit(solution)/shard_map/psum | solution.py:32
  214.1 50.5 %copy-start.3 = (s32[32]{0:T(128)S(1)}, s32[32]{0:T(128)}, u32[]{:S(2)}) copy-start(s32[32]{0:T(128)} %param.8) | copy-start | bytes 388
  214.1 69.4 %copy-start.2 = (f32[16,4,256]{2,1,0:T(4,128)S(1)}, f32[16,4,256]{2,1,0:T(4,128)}, u32[]{:S(2)}) copy-start(f32[16,4,256]{2,1,0:T(4,128)} %param.7) | copy-start | bytes 196612
  214.8 68.8 %reduce-scatter.2.cloned.1.call-start = ((), (), s32[]{:S(2)}) async-start(), calls=%async_computation.6 | async-start | bytes 327680 | tf_op jit(solution)/shard_map/reduce_scatter | solution.py:53
Sparse Core Ops, SparseCore 0:
  11.8 37.0 all-reduce.5
  65.7 33.0 all-reduce.7
  115.4 33.0 all-reduce.9
  165.2 33.0 all-reduce.11
  214.9 33.0 all-reduce.13
  264.7 18.7 reduce-scatter.1
where the time goes:
time: 293 us; the launch traced here: 292 us
  waiting for transfers between devices  178 us (61%)
  blocking collectives  60.6 us (21%)
  between operations  25.9 us (9%)
  matrix products  18.2 us (6%)
  other arithmetic  4.76 us (2%)
  local copies, waits for them, and re-layouts  4.48 us (2%)
    psum x5, waiting for transfers between devices, per_device(): remaining = lax.psum(placed - part_tile, 'row')  159 us
    psum x5, blocking collectives, spread(): return lax.psum(block, axis)  60.6 us
    reduce_scatter x1, waiting for transfers between devices, per_device(): lax.psum_scatter(shaped, 'row', scatter_dimension=2, tiled=True)  18.8 us
    dot_general x5, matrix products, per_device(): lax.dot_general(sent_block, panel_rows, (((1,), (1,)), ((), ())), preferr...  11.2 us
    dot_general x5, matrix products, per_device(): lax.dot_general(remaining, inverse, (((1,), (1,)), ((), ())), precision=l...  7.03 us
  transfers between devices with their start and end apart: 6, of which 6 were waited for; matrix products, arithmetic and copies ran while one was open for 0% of the time, Pallas kernels for 0%

commit v1 on v0

--- a/solution.py
+++ b/solution.py
@@ -2,6 +2,12 @@
 import jax.numpy as jnp
 from jax import lax
 from jax.sharding import PartitionSpec as P
+
+
+def gather_and_add(block, mesh_axis):
+    parts = lax.all_gather(block, mesh_axis, axis=0, tiled=False)
+    result = parts.sum(axis=0)
+    return result
 
 
 def spread(block, axis, owner):
@@ -29,7 +35,7 @@
         placed = lax.dynamic_update_slice_in_dim(
             jnp.zeros((rhs_count, tile_width), jnp.float32), rhs_slice, slice_start, 1
         )
-        remaining = lax.psum(placed - part_tile, "row")
+        remaining = gather_and_add(placed - part_tile, "row")
         inverse = diag_inverse[section].astype(jnp.float32)
         solved = lax.dot_general(
             remaining,

time: 293 us -> 203 us (0.69)
  waiting for transfers between devices: 178 us -> 20.9 us
  blocking collectives: 60.6 us -> 134 us
  matrix products: 18.2 us -> 14.8 us
    psum x5 -> x0, waiting for transfers between devices: 159 us -> none  [per_device(): remaining = lax.psum(placed - part_tile, 'row')]
    all_gather x0 -> x5, blocking collectives: none -> 73.2 us  [gather_and_add(): parts = lax.all_gather(block, mesh_axis, axis=0, tiled=False)]
    dot_general x5, matrix products: 7.03 us -> 3.62 us  [per_device(): lax.dot_general(remaining, inverse, (((1,), (1,)), ((), ())), precision=l...]
  transfers between devices with their start and end apart: 6 -> 1, of which waited for: 6 -> 1; matrix products, arithmetic and copies ran while one was open for 0% -> 0% of each run, Pallas kernels for 0% -> 0%
where the time goes in v1:
time: 203 us; the launch traced here: 202 us
  blocking collectives  134 us (66%)
  between operations  26.4 us (13%)
  waiting for transfers between devices  20.9 us (10%)
  matrix products  14.8 us (7%)
  local copies, waits for them, and re-layouts  3.93 us (2%)
  other arithmetic  2.34 us (1%)
    all_gather x5, blocking collectives, gather_and_add(): parts = lax.all_gather(block, mesh_axis, axis=0, tiled=False)  73.2 us
    psum x5, blocking collectives, spread(): return lax.psum(block, axis)  60.4 us
    reduce_scatter x1, waiting for transfers between devices, per_device(): lax.psum_scatter(shaped, 'row', scatter_dimension=2, tiled=True)  20.9 us
    dot_general x5, matrix products, per_device(): lax.dot_general(sent_block, panel_rows, (((1,), (1,)), ((), ())), preferr...  11.2 us
  transfers between devices with their start and end apart: 1, of which 1 were waited for; matrix products, arithmetic and copies ran while one was open for 0% of the time, Pallas kernels for 0%

profile of v1, /device:TPU:0, one launch (start us, length us, event | category | flops | bytes accessed | tf_op | source)
XLA Modules:
  0.0 202.1 jit_solution(2633194432038082420)
XLA Ops:
  6.5 1.5 fusion.35
  20.8 0.9 copy.30
  21.7 15.7 %all_gather.34 = f32[4,16,1024]{2,1,0:T(8,128)S(1)} all-gather(f32[1,16,1024]{2,1,0:T(8,128)S(1)} %bitcast_dynamic-update-slice_fusion.5), channel_id=1, replica_groups=mesh['row'=4,'col'=8] {'row'}, dimensions={0}, use_global_device_ids=true | all-gather | bytes 327680 | tf_op jit(solution)/shard_map/all_gather | solution.py:8
  37.4 0.7 broadcast_compare_fusion
  38.1 1.6 bitcast_dynamic-update-slice_fusion.4
  39.8 12.2 %psum.35 = bf16[16,256]{1,0:T(8,128)(2,1)S(1)} all-reduce(bf16[16,256]{1,0:T(8,128)(2,1)S(1)} %fusion.30), channel_id=1, replica_groups=mesh['row'=4,'col'=8] {'col'}, use_global_device_ids=true, to_apply=%region_2.3 | all-reduce | flops 4096 | bytes 16384 | tf_op jit(solution)/shard_map/psum | solution.py:15
  52.0 2.2 %fusion.4 = f32[16,4096]{1,0:T(8,128)S(1)} fusion(bf16[16,256]{1,0:T(8,128)(2,1)S(1)} %psum.35, bf16[4096,5,256]{2,0,1:T(8,128)(2,1)} %param.5), kind=kOutput, calls=%fused_computation.8 | convolution fusion | flops 33554432 | bytes 2367488 | tf_op jit(solution)/shard_map/dot_general | solution.py:55
  54.3 14.1 %all-gather = f32[64,1024]{1,0:T(8,128)S(1)} all-gather(f32[16,1024]{1,0:T(8,128)S(1)} %dynamic-slice_subtract_fusion.3), channel_id=2, replica_groups=mesh['row'=4,'col'=8] {'row'}, dimensions={0}, use_global_device_ids=true | all-gather | bytes 327680 | tf_op jit(solution)/shard_map/all_gather | solution.py:8
  69.0 12.1 %psum.36 = bf16[16,256]{1,0:T(8,128)(2,1)S(1)} all-reduce(bf16[16,256]{1,0:T(8,128)(2,1)S(1)} %fusion.31), channel_id=1, replica_groups=mesh['row'=4,'col'=8] {'col'}, use_global_device_ids=true, to_apply=%region_4.5 | all-reduce | flops 4096 | bytes 16384 | tf_op jit(solution)/shard_map/psum | solution.py:15
  81.1 2.2 %convolution_add_fusion.3 = f32[16,4096]{1,0:T(8,128)S(1)} fusion(f32[16,4096]{1,0:T(8,128)S(1)} %fusion.4, bf16[16,256]{1,0:T(8,128)(2,1)S(1)} %psum.36, bf16[4096,5,256]{2,0,1:T(8,128)(2,1)} %param.5), kind=kOutput, calls=%fused_computation.3 | convolution fusion | flops 33619968 | bytes 2629632 | tf_op jit(solution)/shard_map/dot_general | solution.py:55
  83.4 14.5 %all-gather.1 = f32[64,1024]{1,0:T(8,128)S(1)} all-gather(f32[16,1024]{1,0:T(8,128)S(1)} %dynamic-slice_subtract_fusion.2), channel_id=3, replica_groups=mesh['row'=4,'col'=8] {'row'}, dimensions={0}, use_global_device_ids=true | all-gather | bytes 327680 | tf_op jit(solution)/shard_map/all_gather | solution.py:8
  98.5 12.1 %psum.37 = bf16[16,256]{1,0:T(8,128)(2,1)S(1)} all-reduce(bf16[16,256]{1,0:T(8,128)(2,1)S(1)} %fusion.32), channel_id=1, replica_groups=mesh['row'=4,'col'=8] {'col'}, use_global_device_ids=true, to_apply=%region_6.7 | all-reduce | flops 4096 | bytes 16384 | tf_op jit(solution)/shard_map/psum | solution.py:15
  110.6 2.2 %convolution_add_fusion.2 = f32[16,4096]{1,0:T(8,128)S(1)} fusion(f32[16,4096]{1,0:T(8,128)S(1)} %convolution_add_fusion.3, bf16[16,256]{1,0:T(8,128)(2,1)S(1)} %psum.37, bf16[4096,5,256]{2,0,1:T(8,128)(2,1)} %param.5), kind=kOutput, calls=%fused_computation.2 | convolution fusion | flops 33619968 | bytes 2629632 | tf_op jit(solution)/shard_map/dot_general | solution.py:55
  112.9 14.5 %all-gather.2 = f32[64,1024]{1,0:T(8,128)S(1)} all-gather(f32[16,1024]{1,0:T(8,128)S(1)} %dynamic-slice_subtract_fusion.1), channel_id=4, replica_groups=mesh['row'=4,'col'=8] {'row'}, dimensions={0}, use_global_device_ids=true | all-gather | bytes 327680 | tf_op jit(solution)/shard_map/all_gather | solution.py:8
  127.4 0.5 fusion.27
  128.0 12.1 %psum.38 = bf16[16,256]{1,0:T(8,128)(2,1)S(1)} all-reduce(bf16[16,256]{1,0:T(8,128)(2,1)S(1)} %fusion.33), channel_id=1, replica_groups=mesh['row'=4,'col'=8] {'col'}, use_global_device_ids=true, to_apply=%region_8.9 | all-reduce | flops 4096 | bytes 16384 | tf_op jit(solution)/shard_map/psum | solution.py:15
  140.0 2.2 %convolution_add_fusion.1 = f32[16,4096]{1,0:T(8,128)S(1)} fusion(f32[16,4096]{1,0:T(8,128)S(1)} %convolution_add_fusion.2, bf16[16,256]{1,0:T(8,128)(2,1)S(1)} %psum.38, bf16[4096,5,256]{2,0,1:T(8,128)(2,1)} %param.5), kind=kOutput, calls=%fused_computation.1 | convolution fusion | flops 33619968 | bytes 2629632 | tf_op jit(solution)/shard_map/dot_general | solution.py:55
  142.4 14.5 %all-gather.3 = f32[64,1024]{1,0:T(8,128)S(1)} all-gather(f32[16,1024]{1,0:T(8,128)S(1)} %dynamic-slice_subtract_fusion), channel_id=5, replica_groups=mesh['row'=4,'col'=8] {'row'}, dimensions={0}, use_global_device_ids=true | all-gather | bytes 327680 | tf_op jit(solution)/shard_map/all_gather | solution.py:8
  157.5 12.1 %psum.39 = bf16[16,256]{1,0:T(8,128)(2,1)S(1)} all-reduce(bf16[16,256]{1,0:T(8,128)(2,1)S(1)} %fusion.34), channel_id=1, replica_groups=mesh['row'=4,'col'=8] {'col'}, use_global_device_ids=true, to_apply=%region_10.11 | all-reduce | flops 4096 | bytes 16384 | tf_op jit(solution)/shard_map/psum | solution.py:15
  169.5 2.2 %convolution_add_fusion = f32[16,4096]{1,0:T(8,128)S(1)} fusion(f32[16,4096]{1,0:T(8,128)S(1)} %convolution_add_fusion.1, bf16[16,256]{1,0:T(8,128)(2,1)S(1)} %psum.39, bf16[4096,5,256]{2,0,1:T(8,128)(2,1)} %param.5), kind=kOutput, calls=%fused_computation | convolution fusion | flops 33619968 | bytes 2629632 | tf_op jit(solution)/shard_map/dot_general | solution.py:55
  171.8 0.7 copy.41
  172.7 20.9 %reduce-scatter.2.cloned.1.call-done = f32[16,4,256]{2,0,1:T(8,128)} async-done(((f32[16,4,1024]{2,0,1:T(8,128)}), f32[16,4,256]{2,0,1:T(8,128)}) %reduce-scatter.2.cloned.1.call-update) | async-done | bytes 65552 | tf_op jit(solution)/shard_map/reduce_scatter | solution.py:59
  193.6 0.9 subtract_select_fusion
  194.5 0.7 copy.37
  (38 shorter events, 2.5 us)
Async XLA Ops:
  6.5 61.9 %copy-start = (bf16[5,256,1024]{2,1,0:T(8,128)(2,1)S(1)}, bf16[5,256,1024]{2,1,0:T(8,128)(2,1)}, u32[]{:S(2)}) copy-start(bf16[5,256,1024]{2,1,0:T(8,128)(2,1)} %param.6) | copy-start | bytes 7864324
  6.5 187.1 %reduce-scatter.2.cloned.1.call-start = ((), (), s32[]{:S(2)}) async-start(), calls=%async_computation.1 | async-start | bytes 327680 | tf_op jit(solution)/shard_map/reduce_scatter | solution.py:59
  142.3 30.2 %copy-start.2 = (s32[32]{0:T(128)S(1)}, s32[32]{0:T(128)}, u32[]{:S(2)}) copy-start(s32[32]{0:T(128)} %param.8) | copy-start | bytes 388
  142.3 51.3 %copy-start.1 = (f32[16,4,256]{2,1,0:T(4,128)S(1)}, f32[16,4,256]{2,1,0:T(4,128)}, u32[]{:S(2)}) copy-start(f32[16,4,256]{2,1,0:T(4,128)} %param.7) | copy-start | bytes 196612
Sparse Core Ops, SparseCore 0:
  172.6 20.9 reduce-scatter.1
